TPU v7x, 32 devices: a whole 2x2x4 slice. The times are simulated.
32 devices in a mesh: groups: 2 (over x), seq: 16 (over z, y, core).
Axes of the slice: x: 2, y: 2, z: 4, core: 2. Of those that a mesh axis runs over, the one named last changes fastest.
Arguments:
- query: bfloat16 [16, 4096], P('groups'), parts along dimension 0, may hold values from -12 to 12
- new_key: bfloat16 [16, 1024], P('groups'), parts along dimension 0, may hold values from -12 to 12
- new_value: bfloat16 [16, 1024], P('groups'), parts along dimension 0, may hold values from -12 to 12
- cache_keys: bfloat16 [16, 1024, 1024], P('groups', 'seq'), parts along dimension 0, may hold values from -6 to 6
- cache_values: bfloat16 [16, 1024, 1024], P('groups', 'seq'), parts along dimension 0, may hold values from -6 to 6
- cache_lengths: int32 [16], P('groups'), parts along dimension 0, may hold values from 512 to 1024
- residual_input: bfloat16 [16, 4096], P('groups'), parts along dimension 0, may hold values from -6 to 6
- w_out: bfloat16 [4096, 4096], P('seq'), may hold values from -0.09375 to 0.09375
- norm_gain: bfloat16 [4096], replicated, may hold values from 0.099609375 to 1.8984375
- w_router: bfloat16 [4096, 4], replicated, may hold values from -0.09375 to 0.09375
- w_gate: bfloat16 [4096, 28672], P(None, 'seq'), may hold values from -0.09375 to 0.09375
- w_up: bfloat16 [4096, 28672], P(None, 'seq'), may hold values from -0.09375 to 0.09375
- expert_down_weight: bfloat16 [28672, 4096], P('seq'), may hold values from -0.09375 to 0.09375
- expert_ids: int32 [16, 2], P('groups'), parts along dimension 0, may hold values from 0 to 3, all different within a row
Outputs:
- attn_proj: bfloat16 [16, 4096], P('groups', 'seq'), parts along dimension 0
- layer_out: bfloat16 [16, 4096], P('groups', 'seq'), parts along dimension 0
There are 2 independent parts, one for each index of `groups`. A program takes and returns all parts, laid end to end along the dimension named above; an argument that names none is the same for every part. Nothing has to cross between parts.
Inputs may be any that keep to these rules, and one draw needn't show every extreme that they name: Cache positions 0 to cache_lengths[b] - 1 of sequence b are live, the rest are not read; the new key and value are always live. `expert_ids`: the two experts of a token differ.
All inputs are finite; a program needn't handle non-finite values.
Results may differ from a plain program's by a relative error of at most 0.012.
Values sent between devices are 32-bit elements; how exact they have to be, the bound alone decides.
A program may use at most 128 MiB of HBM per device.

v0:
```python
import math

import jax
import jax.numpy as jnp
from jax import lax
from jax.sharding import PartitionSpec as P

HEADS = 32
KV_HEADS = 8
HEAD_DIM = 128
FF = 7168


masked_score = -1e30


def joined(value, axis, join):
    pieces = jax.tree.map(lambda part: lax.all_gather(part, axis), value)
    head = jax.tree.map(lambda part: part[0], pieces)
    tail = jax.tree.map(lambda part: part[1:], pieces)
    so_far, _ = lax.scan(lambda so_far, share: (join(so_far, share), None), head, tail)
    return so_far


def merge_partial_results(first, second):
    first_max, first_sum, first_num = first
    second_max, second_sum, second_num = second
    ceiling = jnp.maximum(first_max, second_max)
    first_scale = jnp.exp(first_max - ceiling)
    second_scale = jnp.exp(second_max - ceiling)
    merged_sum = first_sum * first_scale + second_sum * second_scale
    merged_num = first_num * first_scale[..., None] + second_num * second_scale[..., None]
    return (ceiling, merged_sum, merged_num)


def per_device(
    query,
    new_key,
    new_value,
    cache_keys,
    cache_values,
    cache_lengths,
    residual_input,
    w_out,
    norm_gain,
    w_router,
    w_gate,
    w_up,
    expert_down_weight,
    expert_ids,
):
    seq_count = query.shape[0]
    per_group = HEADS // KV_HEADS
    local_len = cache_keys.shape[1]
    device = lax.axis_index("seq")
    inv_scale = 1.0 / math.sqrt(HEAD_DIM)
    query_vectors = query.reshape(seq_count, KV_HEADS, per_group, HEAD_DIM)
    key_block = cache_keys.reshape(seq_count, local_len, KV_HEADS, HEAD_DIM)
    value_block = cache_values.reshape(seq_count, local_len, KV_HEADS, HEAD_DIM)
    scores = (
        jnp.einsum("bkgd,btkd->bkgt", query_vectors, key_block, preferred_element_type=jnp.float32)
        * inv_scale
    )
    positions = device * local_len + jnp.arange(local_len, dtype=jnp.int32)
    is_live = (positions[None, :] < cache_lengths[:, None])[:, None, None, :]
    scores = jnp.where(is_live, scores, masked_score)
    incoming_key_rows = new_key.reshape(seq_count, KV_HEADS, HEAD_DIM)
    incoming_token_score = (
        jnp.einsum(
            "oqes,oqs->oqe", query_vectors, incoming_key_rows, preferred_element_type=jnp.float32
        )
        * inv_scale
    )
    fresh_value = new_value.astype(jnp.float32).reshape(seq_count, KV_HEADS, 1, HEAD_DIM)
    feat_width = w_out.shape[0]
    feat_start = device * feat_width
    flat_shape = (seq_count, HEADS * HEAD_DIM)
    local_max = jnp.max(scores, axis=-1)
    weights = jnp.where(is_live, jnp.exp(scores - local_max[..., None]), 0.0)
    numerator = jnp.einsum(
        "bkgt,btkd->bkgd",
        weights.astype(jnp.bfloat16),
        value_block,
        preferred_element_type=jnp.float32,
    )
    merged_max, merged_sum, merged_num = joined(
        (local_max, jnp.sum(weights, axis=-1), numerator), "seq", merge_partial_results
    )
    ceiling = jnp.maximum(merged_max, incoming_token_score)
    old_scale = jnp.exp(merged_max - ceiling)
    fresh_weight = jnp.exp(incoming_token_score - ceiling)
    fresh_rounded = lax.optimization_barrier(fresh_weight.astype(jnp.bfloat16)).astype(jnp.float32)
    numerator = merged_num * old_scale[..., None] + fresh_rounded[..., None] * fresh_value
    denominator = merged_sum * old_scale + fresh_weight
    context = (numerator / denominator[..., None]).reshape(flat_shape)
    context_own = lax.dynamic_slice_in_dim(context, feat_start, feat_width, 1).astype(jnp.bfloat16)
    projected = lax.psum(jnp.dot(context_own, w_out, preferred_element_type=jnp.float32), "seq")
    out_width = projected.shape[1] // lax.axis_size("seq")
    out_start = device * out_width
    attn_proj = lax.dynamic_slice_in_dim(projected, out_start, out_width, 1).astype(jnp.bfloat16)
    stream = residual_input.astype(jnp.float32) + projected
    normed = (
        stream
        * lax.rsqrt(jnp.mean(stream * stream, axis=-1, keepdims=True) + 1e-05)
        * norm_gain.astype(jnp.float32)
    )
    normed = normed.astype(jnp.bfloat16)
    logits = jnp.dot(normed, w_router, preferred_element_type=jnp.float32)
    expert_count = w_router.shape[1]
    picks = expert_ids[:, :, None] == jnp.arange(expert_count, dtype=jnp.int32)[None, None, :]
    chosen = jnp.sum(jnp.where(picks, logits[:, None, :], 0.0), axis=-1)
    first_gate = jax.nn.sigmoid(chosen[:, 0] - chosen[:, 1])
    gate_pair = jnp.stack([first_gate, 1.0 - first_gate], axis=1)
    own_expert = device * w_gate.shape[1] // FF
    route_weight = jnp.sum(jnp.where(expert_ids == own_expert, gate_pair, 0.0), axis=1)
    gate_part = jnp.dot(normed, w_gate, preferred_element_type=jnp.float32)
    up_projection_share = jnp.dot(normed, w_up, preferred_element_type=jnp.float32)
    hidden = (jax.nn.silu(gate_part) * up_projection_share).astype(jnp.bfloat16)
    term = lax.dot_general(
        expert_down_weight, hidden, (((0,), (1,)), ((), ())), preferred_element_type=jnp.float32
    )
    moe_rows = lax.psum_scatter(
        term * route_weight[None, :], "seq", scatter_dimension=0, tiled=True
    )
    stream_own = lax.dynamic_slice_in_dim(stream, out_start, out_width, 1)
    layer_out = (stream_own + moe_rows.T).astype(jnp.bfloat16)
    return (attn_proj, layer_out)


def solution(mesh):
    placed = (
        P("groups", None),
        P("groups", None),
        P("groups", None),
        P("groups", "seq", None),
        P("groups", "seq", None),
        P("groups"),
        P("groups", None),
        P("seq", None),
        P(),
        P(),
        P(None, "seq"),
        P(None, "seq"),
        P("seq", None),
        P("groups", None),
    )
    return jax.shard_map(
        per_device,
        mesh=mesh,
        in_specs=placed,
        out_specs=(P("groups", "seq"), P("groups", "seq")),
        check_vma=False,
    )
```

profile of v0, /device:TPU:0, one launch (start us, length us, event | category | flops | bytes accessed | tf_op | source)
XLA Modules:
  0.0 263.8 jit_solution(7450599788652511796)
XLA Ops:
  7.3 0.9 broadcast_compare_fusion
  8.1 2.0 fusion.38
  10.1 1.7 fusion.7
  11.8 0.7 copy.51
  13.1 24.1 %all-gather.1 = f32[128,8,4]{1,2,0:T(4,128)S(1)} all-gather(f32[8,8,4]{1,2,0:T(4,128)S(1)} %copy.49), channel_id=3, replica_groups=mesh['groups'=2,'seq'=16] {'seq'}, dimensions={0}, use_global_device_ids=true | all-gather | bytes 17408 | tf_op jit(solution)/shard_map/all_gather | solution.py:18
  37.2 18.7 %all-gather = f32[128,8,4]{1,2,0:T(4,128)S(1)} all-gather(f32[8,8,4]{1,2,0:T(4,128)S(1)} %copy.48), channel_id=2, replica_groups=mesh['groups'=2,'seq'=16] {'seq'}, dimensions={0}, use_global_device_ids=true | all-gather | bytes 17408 | tf_op jit(solution)/shard_map/all_gather | solution.py:18
  56.0 1.0 fusion.23
  57.2 0.7 bitcast_convert_fusion
  57.9 0.9 slice.40
  58.9 3.0 %slice.43 = f32[120,8,4,128]{3,1,2,0:T(8,128)} slice(f32[128,8,4,128]{3,1,2,0:T(8,128)} %all-gather.5.cloned.1.call-done), slice={[8:128], [0:8], [0:4], [0:128]} | slice | bytes 3932160 | tf_op jit(solution)/shard_map/slice | solution.py:20
  61.9 24.5 %while.14 = (s32[]{:T(128)}, f32[8,8,4]{1,2,0:T(4,128)S(1)}, f32[8,8,4]{1,2,0:T(4,128)S(1)}, f32[8,8,4,128]{3,2,1,0:T(4,128)S(1)}, f32[15,8,8,4]{2,3,1,0:T(4,128...) while((s32[]{:T(128)}, f32[8,8,4]{1,2,0:T(4,128)S(1)}, ...), condition=%wide.region_3.4_spmd, body=%wide.region_2.3_spmd.sunk | while | flops 99842 | bytes 669797 | solution.py:21
  62.1 0.9 constant_dynamic-slice_fusion.2
  63.0 0.4 fusion.54
  63.8 0.9 constant_dynamic-slice_fusion.2
  64.7 0.4 fusion.54
  65.4 0.9 constant_dynamic-slice_fusion.2
  66.3 0.4 fusion.54
  67.0 0.9 constant_dynamic-slice_fusion.2
  68.0 0.4 fusion.54
  68.7 0.9 constant_dynamic-slice_fusion.2
  69.6 0.4 fusion.54
  70.3 0.9 constant_dynamic-slice_fusion.2
  71.2 0.4 fusion.54
  72.0 0.9 constant_dynamic-slice_fusion.2
  72.9 0.4 fusion.54
  73.6 0.9 constant_dynamic-slice_fusion.2
  74.5 0.4 fusion.54
  75.2 0.9 constant_dynamic-slice_fusion.2
  76.9 0.9 constant_dynamic-slice_fusion.2
  77.8 0.4 fusion.54
  78.5 0.9 constant_dynamic-slice_fusion.2
  79.4 0.4 fusion.54
  80.1 0.9 constant_dynamic-slice_fusion.2
  81.1 0.4 fusion.54
  81.8 0.9 constant_dynamic-slice_fusion.2
  82.7 0.4 fusion.54
  83.4 0.9 constant_dynamic-slice_fusion.2
  84.3 0.4 fusion.54
  85.1 0.9 constant_dynamic-slice_fusion.2
  86.0 0.4 fusion.54
  87.1 1.0 fusion.31
  88.3 87.4 %all-reduce.2.cloned.1.call-done = f32[8,4096]{1,0:T(8,128)} async-done(((f32[8,4096]{1,0:T(8,128)}), f32[8,4096]{1,0:T(8,128)}) %all-reduce.2.cloned.1.call-update) | async-done | bytes 131088 | tf_op jit(solution)/shard_map/psum | solution.py:97
  175.8 1.1 multiply_reduce_fusion
  177.1 7.2 %fusion.39 = f32[8,1792]{1,0:T(8,128)S(1)} fusion(bf16[8,4096]{1,0:T(8,128)(2,1)S(1)} %multiply_convert_fusion, bf16[4096,1792]{1,0:T(8,128)(2,1)} %param.26), kind=kOutput, calls=%fused_computation.67 | convolution fusion | flops 117440512 | bytes 14802944 | tf_op jit(solution)/shard_map/dot_general | solution.py:116
  184.3 14.3 %fusion.4 = f32[4096,8]{0,1:T(8,128)} fusion(bf16[1792,4096]{1,0:T(8,128)(2,1)} %param.28, bf16[8,4096]{1,0:T(8,128)(2,1)S(1)} %multiply_convert_fusion, bf16[4096,1792]{1,0:T(8,128)(2,1)} %param.27, f32[8]{0:T(128)S(1)} %fusion.32, f32[8,1792]{1,0:T(8,128)S(1)} %fusion.39), kind=kOutput, calls=%fused_computation.11 | convolution fusion | flops 234999808 | bytes 29614112 | tf_op jit(solution)/shard_map/dot_general | solution.py:119
  198.6 1.3 dynamic-slice_convert_fusion
  199.9 56.0 %reduce-scatter.2.cloned.1.call-done = f32[256,8]{0,1:T(8,128)} async-done(((f32[4096,8]{0,1:T(8,128)}), f32[256,8]{0,1:T(8,128)}) %reduce-scatter.2.cloned.1.call-update) | async-done | bytes 8208 | tf_op jit(solution)/shard_map/reduce_scatter | solution.py:122
  255.9 1.3 fusion.30
  (87 shorter events, 6.6 us)
Async XLA Ops:
  7.2 80.0 %copy-start = (bf16[256,4096]{1,0:T(8,128)(2,1)S(1)}, bf16[256,4096]{1,0:T(8,128)(2,1)}, u32[]{:S(2)}) copy-start(bf16[256,4096]{1,0:T(8,128)(2,1)} %param.23) | copy-start | bytes 6291460
  7.2 81.1 %copy-start.2 = (bf16[4096]{0:T(1024)(128)(2,1)S(1)}, bf16[4096]{0:T(1024)(128)(2,1)}, u32[]{:S(2)}) copy-start(bf16[4096]{0:T(1024)(128)(2,1)} %param.24) | copy-start | bytes 24580
  7.2 168.6 %copy-start.1 = (bf16[8,4096]{1,0:T(8,128)(2,1)S(1)}, bf16[8,4096]{1,0:T(8,128)(2,1)}, u32[]{:S(2)}) copy-start(bf16[8,4096]{1,0:T(8,128)(2,1)} %param.22) | copy-start | bytes 196612
  7.2 169.7 %copy-start.4 = (bf16[4096,4]{0,1:T(4,128)(2,1)S(1)}, bf16[4096,4]{0,1:T(4,128)(2,1)}, u32[]{:S(2)}) copy-start(bf16[4096,4]{0,1:T(4,128)(2,1)} %param.25) | copy-start | bytes 98308
  7.2 169.9 %copy-start.3 = (s32[8,2]{0,1:T(2,128)S(1)}, s32[8,2]{0,1:T(2,128)}, u32[]{:S(2)}) copy-start(s32[8,2]{0,1:T(2,128)} %param.29) | copy-start | bytes 196
  7.2 50.7 %all-gather.5.cloned.1.call-start = ((), (), s32[]{:S(2)}) async-start(), calls=%async_computation.3 | async-start | bytes 2228224 | tf_op jit(solution)/shard_map/all_gather | solution.py:18
  12.5 163.2 %all-reduce.2.cloned.1.call-start = ((), (), s32[]{:S(2)}) async-start(), calls=%async_computation.1 | async-start | bytes 262144 | tf_op jit(solution)/shard_map/psum | solution.py:97
  88.2 167.7 %reduce-scatter.2.cloned.1.call-start = ((), (), s32[]{:S(2)}) async-start(), calls=%async_computation.2 | async-start | bytes 139264 | tf_op jit(solution)/shard_map/reduce_scatter | solution.py:122
Sparse Core Ops, SparseCore 0:
  12.6 44.5 all-gather.4
  88.3 87.3 all-reduce.1
  198.7 57.1 reduce-scatter.1
where the time goes:
time: 265 us; the launch traced here: 264 us
  waiting for transfers between devices  144 us (54%)
  blocking collectives  42.9 us (16%)
  matrix products  27.3 us (10%)
  local copies, waits for them, and re-layouts  24.1 us (9%)
  between operations  14 us (5%)
  other arithmetic  11.7 us (4%)
    psum x1, waiting for transfers between devices, per_device(): lax.psum(jnp.dot(context_own, w_out, preferred_element_type=jnp.float32),...  87.4 us
    reduce_scatter x1, waiting for transfers between devices, per_device(): lax.psum_scatter(term * route_weight[None, :], 'seq', scatter_dimension=0...  56 us
    all_gather x2, blocking collectives, joined(): pieces = jax.tree.map(lambda part: lax.all_gather(part, axis), value)  42.9 us
    dot_general x1, matrix products, per_device(): lax.dot_general(expert_down_weight, hidden, (((0,), (1,)), ((), ())), pre...  14.3 us
    dynamic_slice x15, local copies, waits for them, and re-layouts, joined(): lax.scan(lambda so_far, share: (join(so_far, share), None), head, tail)  13.7 us
    dot_general x1, matrix products, per_device(): gate_part = jnp.dot(normed, w_gate, preferred_element_type=jnp.float32)  7.18 us
    add x15, other arithmetic, merge_partial_results(): first_num * first_scale[..., None] + second_num * second_scale[..., None]  6.37 us
  transfers between devices with their start and end apart: 3, of which 2 were waited for; matrix products, arithmetic and copies ran while one was open for 1% of the time, Pallas kernels for 0%

commit v1 on v0

--- a/solution.py
+++ b/solution.py
@@ -1,8 +1,11 @@
+import functools
 import math
 
 import jax
 import jax.numpy as jnp
 from jax import lax
+from jax.experimental import pallas as pl
+from jax.experimental.pallas import tpu as pltpu
 from jax.sharding import PartitionSpec as P
 
 HEADS = 32
@@ -127,6 +130,387 @@
     return (attn_proj, layer_out)
 
 
+def layer_kernel(
+    n,
+    lengths_ref,
+    ids_ref,
+    query_hbm,
+    new_key_hbm,
+    new_value_hbm,
+    keys_hbm,
+    values_hbm,
+    residual_hbm,
+    w_out_hbm,
+    gain_hbm,
+    router_hbm,
+    gate_hbm,
+    up_hbm,
+    down_hbm,
+    attn_out,
+    layer_out,
+    query,
+    new_key,
+    new_value,
+    keys,
+    values,
+    residual,
+    w_out,
+    gain,
+    router,
+    w_gate,
+    w_up,
+    w_down,
+    send_ctx,
+    recv_ctx,
+    send_proj,
+    recv_proj,
+    gathered,
+    send_moe,
+    recv_moe,
+    normed_ref,
+    hidden_ref,
+    small_sem,
+    gate_sem,
+    up_sem,
+    down_sem,
+    send_sem,
+    recv_sem,
+):
+    f32, bf16 = jnp.float32, jnp.bfloat16
+    me = lax.axis_index("seq")
+    seqs = query.shape[0]
+    local_len = keys.shape[1]
+    per_group = HEADS // KV_HEADS
+    width = w_out.shape[0]
+    own_heads = width // HEAD_DIM
+    ff_local = w_gate.shape[1]
+    inv_scale = 1.0 / math.sqrt(HEAD_DIM)
+
+    small = [
+        pltpu.make_async_copy(src, dst, small_sem.at[i])
+        for i, (src, dst) in enumerate(
+            (
+                (query_hbm, query),
+                (keys_hbm, keys),
+                (values_hbm, values),
+                (new_key_hbm, new_key),
+                (new_value_hbm, new_value),
+                (w_out_hbm, w_out),
+                (residual_hbm, residual),
+                (gain_hbm, gain),
+                (router_hbm, router),
+            )
+        )
+    ]
+    for copy in small:
+        copy.start()
+    big = []
+    for src, dst, sems in (
+        (gate_hbm, w_gate, gate_sem),
+        (up_hbm, w_up, up_sem),
+        (down_hbm, w_down, down_sem),
+    ):
+        parts = sems.shape[0]
+        rows = src.shape[0] // parts
+        copies = [
+            pltpu.make_async_copy(
+                src.at[pl.ds(i * rows, rows)], dst.at[pl.ds(i * rows, rows)], sems.at[i]
+            )
+            for i in range(parts)
+        ]
+        for copy in copies:
+            copy.start()
+        big.append(copies)
+
+    barrier = pltpu.get_barrier_semaphore()
+
+    def greet(i, carry):
+        pl.semaphore_signal(barrier, inc=1, device_id={"seq": lax.rem(me + i, n)})
+        return carry
+
+    lax.fori_loop(1, n, greet, 0)
+
+    def exchange(phase, src, dst, peer, slot):
+        return pltpu.make_async_remote_copy(
+            src_ref=src,
+            dst_ref=dst.at[slot],
+            send_sem=send_sem.at[phase, peer],
+            recv_sem=recv_sem.at[phase, slot],
+            device_id={"seq": peer},
+        )
+
+    def wait_all(phase, dst):
+        def step(i, carry):
+            peer = lax.rem(me + i, n)
+            exchange(phase, dst.at[peer], dst, peer, peer).wait_recv()
+            return carry
+
+        lax.fori_loop(1, n, step, 0)
+
+    rows = per_group * seqs
+    cols = seqs * local_len
+    row_seq = lax.rem(lax.broadcasted_iota(jnp.int32, (rows, 1), 0), seqs)
+    row_len = jnp.zeros((rows, 1), jnp.int32)
+    for b in range(seqs):
+        row_len = jnp.where(row_seq == b, lengths_ref[b], row_len)
+    offset = lax.broadcasted_iota(jnp.int32, (rows, cols), 1) - row_seq * local_len
+    valid = (offset >= 0) & (offset < jnp.minimum(row_len - me * local_len, local_len))
+    lane = lax.broadcasted_iota(jnp.int32, (rows, HEAD_DIM), 1)
+
+    for copy in small[:3]:
+        copy.wait()
+    stats = [None] * HEADS
+    for k in range(KV_HEADS):
+        span = slice(k * HEAD_DIM, (k + 1) * HEAD_DIM)
+        grouped = jnp.concatenate(
+            [
+                query[:, (k * per_group + g) * HEAD_DIM : (k * per_group + g + 1) * HEAD_DIM].astype(f32)
+                for g in range(per_group)
+            ],
+            axis=0,
+        ).astype(bf16)
+        key_block = keys[:, :, span].reshape(cols, HEAD_DIM)
+        value_block = values[:, :, span].reshape(cols, HEAD_DIM)
+        scores = (
+            lax.dot_general(
+                grouped, key_block, (((1,), (1,)), ((), ())), preferred_element_type=f32
+            )
+            * inv_scale
+        )
+        scores = jnp.where(valid, scores, masked_score)
+        top = jnp.max(scores, axis=1, keepdims=True)
+        weights = jnp.where(valid, jnp.exp(scores - top), 0.0)
+        total = jnp.sum(weights, axis=1, keepdims=True)
+        numerator = jnp.dot(weights.astype(bf16), value_block, preferred_element_type=f32)
+        for g in range(per_group):
+            head = k * per_group + g
+            peer, part = head // own_heads, head % own_heads
+            part_rows = slice(g * seqs, (g + 1) * seqs)
+            send_ctx[peer, :, part * HEAD_DIM : (part + 1) * HEAD_DIM] = numerator[part_rows]
+            stats[head] = jnp.where(
+                lane[:seqs] == 2 * part,
+                top[part_rows],
+                jnp.where(lane[:seqs] == 2 * part + 1, total[part_rows], 0.0),
+            )
+    for peer in range(n):
+        block = stats[peer * own_heads]
+        for part in range(1, own_heads):
+            block = block + stats[peer * own_heads + part]
+        send_ctx[peer, :, width:] = block
+
+    pl.semaphore_wait(barrier, n - 1)
+
+    def send_context(i, carry):
+        peer = lax.rem(me + i, n)
+        exchange(0, send_ctx.at[peer], recv_ctx, peer, me).start()
+        return carry
+
+    lax.fori_loop(1, n, send_context, 0)
+    recv_ctx[pl.ds(me, 1)] = send_ctx[pl.ds(me, 1)]
+
+    for copy in small[3:5]:
+        copy.wait()
+    fresh = []
+    for part in range(own_heads):
+        head = me * own_heads + part
+        kv = head // per_group
+        at = pl.ds(pl.multiple_of(kv * HEAD_DIM, HEAD_DIM), HEAD_DIM)
+        q_at = pl.ds(pl.multiple_of(head * HEAD_DIM, HEAD_DIM), HEAD_DIM)
+        score = (
+            jnp.sum(query[:, q_at].astype(f32) * new_key[:, at].astype(f32), axis=1, keepdims=True)
+            * inv_scale
+        )
+        fresh.append((score, new_value[:, at].astype(f32)))
+
+    wait_all(0, recv_ctx)
+    pieces = []
+    for part in range(own_heads):
+        score, value = fresh[part]
+        tops = recv_ctx[:, :, width + 2 * part : width + 2 * part + 1]
+        totals = recv_ctx[:, :, width + 2 * part + 1 : width + 2 * part + 2]
+        ceiling = jnp.maximum(jnp.max(tops, axis=0), score)
+        scale = jnp.exp(tops - ceiling[None])
+        new_weight = jnp.exp(score - ceiling)
+        denominator = jnp.sum(totals * scale, axis=0) + new_weight
+        numerator = jnp.sum(
+            recv_ctx[:, :, part * HEAD_DIM : (part + 1) * HEAD_DIM] * scale, axis=0
+        )
+        numerator = numerator + new_weight.astype(bf16).astype(f32) * value
+        pieces.append(numerator / denominator)
+    context = jnp.concatenate(pieces, axis=1).astype(bf16)
+
+    small[5].wait()
+
+    def project(peer):
+        at = pl.ds(pl.multiple_of(peer * width, width), width)
+        return jnp.dot(context, w_out[:, at], preferred_element_type=f32)
+
+    def send_projected(i, carry):
+        peer = lax.rem(me + i, n)
+        send_proj[peer] = project(peer)
+        exchange(1, send_proj.at[peer], recv_proj, peer, me).start()
+        return carry
+
+    lax.fori_loop(1, n, send_projected, 0)
+    recv_proj[me] = project(me)
+    for copy in small[6:]:
+        copy.wait()
+    wait_all(1, recv_proj)
+    projected = jnp.sum(recv_proj[...], axis=0)
+    gathered[me] = projected
+
+    def send_gathered(i, carry):
+        peer = lax.rem(me + i, n)
+        exchange(2, gathered.at[me], gathered, peer, me).start()
+        return carry
+
+    lax.fori_loop(1, n, send_gathered, 0)
+    attn_out[...] = projected.astype(bf16)
+    own_at = pl.ds(pl.multiple_of(me * width, width), width)
+    stream_own = residual[:, own_at].astype(f32) + projected
+    wait_all(2, gathered)
+
+    stream = [
+        gathered[p] + residual[:, p * width : (p + 1) * width].astype(f32) for p in range(n)
+    ]
+    squares = stream[0] * stream[0]
+    for p in range(1, n):
+        squares = squares + stream[p] * stream[p]
+    inv_rms = lax.rsqrt(jnp.sum(squares, axis=1, keepdims=True) / (n * width) + 1e-05)
+    for p in range(n):
+        at = slice(p * width, (p + 1) * width)
+        normed_ref[:, at] = (stream[p] * inv_rms * gain[:, at].astype(f32)).astype(bf16)
+
+    normed = normed_ref[...]
+    logits = lax.dot_general(
+        normed, router[...], (((1,), (1,)), ((), ())), preferred_element_type=f32
+    )
+    expert = lax.broadcasted_iota(jnp.int32, logits.shape, 1)
+    token = lax.broadcasted_iota(jnp.int32, (seqs, 1), 0)
+    first_id = jnp.zeros((seqs, 1), jnp.int32)
+    second_id = jnp.zeros((seqs, 1), jnp.int32)
+    for b in range(seqs):
+        first_id = jnp.where(token == b, ids_ref[b, 0], first_id)
+        second_id = jnp.where(token == b, ids_ref[b, 1], second_id)
+    first_logit = jnp.sum(jnp.where(expert == first_id, logits, 0.0), axis=1, keepdims=True)
+    second_logit = jnp.sum(jnp.where(expert == second_id, logits, 0.0), axis=1, keepdims=True)
+    first_gate = 1.0 / (1.0 + jnp.exp(second_logit - first_logit))
+    own_expert = me * ff_local // FF
+    route = jnp.where(first_id == own_expert, first_gate, 0.0) + jnp.where(
+        second_id == own_expert, 1.0 - first_gate, 0.0
+    )
+
+    for copies in big[:2]:
+        for copy in copies:
+            copy.wait()
+    tile = 256
+
+    def hidden_step(j, carry):
+        at = pl.ds(pl.multiple_of(j * tile, tile), tile)
+        gate_part = jnp.dot(normed_ref[...], w_gate[:, at], preferred_element_type=f32)
+        up_part = jnp.dot(normed_ref[...], w_up[:, at], preferred_element_type=f32)
+        hidden_ref[:, at] = (gate_part / (1.0 + jnp.exp(-gate_part)) * up_part).astype(bf16)
+        return carry
+
+    lax.fori_loop(0, ff_local // tile, hidden_step, 0)
+    for copy in big[2]:
+        copy.wait()
+
+    def contribution(peer):
+        at = pl.ds(pl.multiple_of(peer * width, width), width)
+        return jnp.dot(hidden_ref[...], w_down[:, at], preferred_element_type=f32) * route
+
+    def send_contribution(i, carry):
+        peer = lax.rem(me + i, n)
+        send_moe[peer] = contribution(peer)
+        exchange(3, send_moe.at[peer], recv_moe, peer, me).start()
+        return carry
+
+    lax.fori_loop(1, n, send_contribution, 0)
+    recv_moe[me] = contribution(me)
+    wait_all(3, recv_moe)
+    layer_out[...] = (stream_own + jnp.sum(recv_moe[...], axis=0)).astype(bf16)
+
+    def finish(i, carry):
+        peer = lax.rem(me + i, n)
+        exchange(0, send_ctx.at[peer], recv_ctx, peer, me).wait_send()
+        exchange(1, send_proj.at[peer], recv_proj, peer, me).wait_send()
+        exchange(2, gathered.at[me], gathered, peer, me).wait_send()
+        exchange(3, send_moe.at[peer], recv_moe, peer, me).wait_send()
+        return carry
+
+    lax.fori_loop(1, n, finish, 0)
+
+
+def fused_device(n, *args):
+    (
+        query,
+        new_key,
+        new_value,
+        cache_keys,
+        cache_values,
+        cache_lengths,
+        residual_input,
+        w_out,
+        norm_gain,
+        w_router,
+        w_gate,
+        w_up,
+        expert_down_weight,
+        expert_ids,
+    ) = args
+    seqs, features = residual_input.shape
+    width = w_out.shape[0]
+    if width % HEAD_DIM or w_gate.shape[1] % 256 or width * n != features or cache_keys.shape[1] % 16:
+        return per_device(*args)
+    f32, bf16 = jnp.float32, jnp.bfloat16
+    operands = (
+        query,
+        new_key,
+        new_value,
+        cache_keys,
+        cache_values,
+        residual_input,
+        w_out,
+        norm_gain.reshape(1, features),
+        w_router.T,
+        w_gate,
+        w_up,
+        expert_down_weight,
+    )
+    packet = (n, seqs, width + HEAD_DIM)
+    block = (n, seqs, width)
+    out = jax.ShapeDtypeStruct((seqs, width), bf16)
+    return pl.pallas_call(
+        functools.partial(layer_kernel, n),
+        out_shape=(out, out),
+        in_specs=[pl.BlockSpec(memory_space=pltpu.SMEM)] * 2
+        + [pl.BlockSpec(memory_space=pl.ANY)] * len(operands),
+        out_specs=(pl.BlockSpec(memory_space=pltpu.VMEM),) * 2,
+        scratch_shapes=[pltpu.VMEM(x.shape, x.dtype) for x in operands]
+        + [
+            pltpu.VMEM(packet, f32),
+            pltpu.VMEM(packet, f32),
+            pltpu.VMEM(block, f32),
+            pltpu.VMEM(block, f32),
+            pltpu.VMEM(block, f32),
+            pltpu.VMEM(block, f32),
+            pltpu.VMEM(block, f32),
+            pltpu.VMEM((seqs, features), bf16),
+            pltpu.VMEM((seqs, w_gate.shape[1]), bf16),
+            pltpu.SemaphoreType.DMA((9,)),
+            pltpu.SemaphoreType.DMA((4,)),
+            pltpu.SemaphoreType.DMA((4,)),
+            pltpu.SemaphoreType.DMA((4,)),
+            pltpu.SemaphoreType.DMA((4, n)),
+            pltpu.SemaphoreType.DMA((4, n)),
+        ],
+        compiler_params=pltpu.CompilerParams(
+            collective_id=0, has_side_effects=True, vmem_limit_bytes=60 * 1024 * 1024
+        ),
+    )(cache_lengths, expert_ids, *operands)
+
+
 def solution(mesh):
     placed = (
         P("groups", None),
@@ -145,7 +529,7 @@
         P("groups", None),
     )
     return jax.shard_map(
-        per_device,
+        functools.partial(fused_device, mesh.shape["seq"]),
         mesh=mesh,
         in_specs=placed,
         out_specs=(P("groups", "seq"), P("groups", "seq")),

time: 265 us -> 43.7 us (0.16)
  waiting for transfers between devices: 144 us -> 0 us
  blocking collectives: 42.9 us -> 0 us
  Pallas kernels: 0 us -> 37.6 us
  matrix products: 27.3 us -> 0 us
  local copies, waits for them, and re-layouts: 24.1 us -> 5.19 us
  between operations: 14 us -> 0.64 us
  other arithmetic: 11.7 us -> 0 us
    psum x1 -> x0, waiting for transfers between devices: 87.4 us -> none  [per_device(): lax.psum(jnp.dot(context_own, w_out, preferred_element_type=jnp.float32),...]
    reduce_scatter x1 -> x0, waiting for transfers between devices: 56 us -> none  [per_device(): lax.psum_scatter(term * route_weight[None, :], 'seq', scatter_dimension=0...]
    all_gather x2 -> x0, blocking collectives: 42.9 us -> none  [joined(): pieces = jax.tree.map(lambda part: lax.all_gather(part, axis), value)]
    pallas_call x0 -> x1, Pallas kernels: none -> 37.6 us  [fused_device(): pl.pallas_call(functools.partial(layer_kernel, n), out_shape=(out, out),...]
    dot_general x7 -> x0, matrix products: 27.3 us -> none  [the longest x1 14.3 us: per_device(): lax.dot_general(expert_down_weight, hidden, (((0,), (1,)), ((), ())), pre...]
    dynamic_slice x15 -> x0, local copies, waits for them, and re-layouts: 13.7 us -> none  [joined(): lax.scan(lambda so_far, share: (join(so_far, share), None), head, tail)]
    add x31 -> x0, other arithmetic: 6.98 us -> none  [the longest x15 6.37 us: merge_partial_results(): first_num * first_scale[..., None] + second_num * second_scale[..., None]]
    slice x6 -> x0, local copies, waits for them, and re-layouts: 3.91 us -> none  [the longest x3 3 us: joined(): tail = jax.tree.map(lambda part: part[1:], pieces)]
  transfers between devices with their start and end apart: 3 -> 0, of which waited for: 2 -> 0; matrix products, arithmetic and copies ran while one was open for 1% -> 0% of each run, Pallas kernels for 0% -> 0%
where the time goes in v1:
time: 43.7 us; the launch traced here: 43.4 us
  Pallas kernels  37.6 us (86%)
  local copies, waits for them, and re-layouts  5.19 us (12%)
  between operations  0.64 us (1%)
    pallas_call x1, Pallas kernels, fused_device(): pl.pallas_call(functools.partial(layer_kernel, n), out_shape=(out, out),...  37.6 us
    unnamed x3, local copies, waits for them, and re-layouts  3.88 us
    reshape x1, local copies, waits for them, and re-layouts, fused_device(): norm_gain.reshape(1, features)  1.31 us

profile of v1, /device:TPU:0, one launch (start us, length us, event | category | flops | bytes accessed | tf_op | source)
XLA Modules:
  0.0 43.4 jit_solution(9504533855327725094)
XLA Ops:
  0.6 1.3 %copy.16.ids_ref = s32[8,2]{1,0:T(8,128)} copy(s32[8,2]{0,1:T(2,128)} %param.27) | data formatting | bytes 128 | tf_op args[13]
  2.0 1.3 %reshape.7.gain_hbm = bf16[1,4096]{1,0:T(2,128)(2,1)} reshape(bf16[4096]{0:T(1024)(128)(2,1)} %param.22) | data formatting | bytes 16384 | tf_op jit(solution)/shard_map/reshape | solution.py:475
  3.3 37.6 %shard_map.149 = (bf16[8,256]{1,0:T(8,128)(2,1)}, bf16[8,256]{1,0:T(8,128)(2,1)}) custom-call(s32[8]{0:T(128)} %lengths_ref.1, s32[8,2]{1,0:T(8,128)} %copy.16.ids_ref, bf16[8,4096]{1,0:T(8,128)(2,1)} %query_hbm.1, bf16[8,1024]{1,0:T(8,128)(2,1)} %new_key_hbm.1, bf16[8,1024]{1,0:T(8,128)(2,1)} %new_value_hbm.1, bf16[8,64,1024]{2,1,0:T(8,128)(2,1)} %keys_hbm.1, ...), custom_call_target="tpu_custom_call" | custom-call | tf_op jit(solution)/shard_map/pallas_call | solution.py:484
  40.9 1.3 %copy.19 = bf16[8,256]{1,0:T(8,128)(2,1)} copy(bf16[8,256]{1,0:T(8,128)(2,1)} %get-tuple-element.4) | data formatting | bytes 8192
  42.1 1.3 %copy.20 = bf16[8,256]{1,0:T(8,128)(2,1)} copy(bf16[8,256]{1,0:T(8,128)(2,1)} %get-tuple-element.5) | data formatting | bytes 8192

commit v2 on v1

--- a/solution.py
+++ b/solution.py
@@ -128,6 +128,17 @@
     stream_own = lax.dynamic_slice_in_dim(stream, out_start, out_width, 1)
     layer_out = (stream_own + moe_rows.T).astype(jnp.bfloat16)
     return (attn_proj, layer_out)
+
+
+GROUP = 4
+
+
+def xor_index(first, second, limit):
+    result, bit = 0, 1
+    while bit < limit:
+        result = result + (first // bit + second // bit) % 2 * bit
+        bit *= 2
+    return result
 
 
 def layer_kernel(
@@ -167,7 +178,9 @@
     gathered,
     send_moe,
     recv_moe,
-    normed_ref,
+    scaled_ref,
+    acc_gate,
+    acc_up,
     hidden_ref,
     small_sem,
     gate_sem,
@@ -241,7 +254,7 @@
 
     def wait_all(phase, dst):
         def step(i, carry):
-            peer = lax.rem(me + i, n)
+            peer = xor_index(me, i, n)
             exchange(phase, dst.at[peer], dst, peer, peer).wait_recv()
             return carry
 
@@ -301,7 +314,7 @@
     pl.semaphore_wait(barrier, n - 1)
 
     def send_context(i, carry):
-        peer = lax.rem(me + i, n)
+        peer = xor_index(me, n - i, n)
         exchange(0, send_ctx.at[peer], recv_ctx, peer, me).start()
         return carry
 
@@ -341,18 +354,17 @@
 
     small[5].wait()
 
-    def project(peer):
-        at = pl.ds(pl.multiple_of(peer * width, width), width)
-        return jnp.dot(context, w_out[:, at], preferred_element_type=f32)
+    products = jnp.dot(context, w_out[...], preferred_element_type=f32)
+    for p in range(n):
+        send_proj[p] = products[:, p * width : (p + 1) * width]
 
     def send_projected(i, carry):
-        peer = lax.rem(me + i, n)
-        send_proj[peer] = project(peer)
+        peer = xor_index(me, n - i, n)
         exchange(1, send_proj.at[peer], recv_proj, peer, me).start()
         return carry
 
     lax.fori_loop(1, n, send_projected, 0)
-    recv_proj[me] = project(me)
+    recv_proj[pl.ds(me, 1)] = send_proj[pl.ds(me, 1)]
     for copy in small[6:]:
         copy.wait()
     wait_all(1, recv_proj)
@@ -360,7 +372,7 @@
     gathered[me] = projected
 
     def send_gathered(i, carry):
-        peer = lax.rem(me + i, n)
+        peer = xor_index(me, n - i, n)
         exchange(2, gathered.at[me], gathered, peer, me).start()
         return carry
 
@@ -368,30 +380,59 @@
     attn_out[...] = projected.astype(bf16)
     own_at = pl.ds(pl.multiple_of(me * width, width), width)
     stream_own = residual[:, own_at].astype(f32) + projected
-    wait_all(2, gathered)
-
-    stream = [
-        gathered[p] + residual[:, p * width : (p + 1) * width].astype(f32) for p in range(n)
-    ]
-    squares = stream[0] * stream[0]
-    for p in range(1, n):
-        squares = squares + stream[p] * stream[p]
+    for copies in big[:2]:
+        for copy in copies:
+            copy.wait()
+
+    groups = n // GROUP
+    span = GROUP * width
+    own_group = me // GROUP
+    logit_shape = (seqs, router.shape[0])
+
+    def absorb(i, carry):
+        squares, logits = carry
+        group = xor_index(own_group, i, groups)
+        for q in range(GROUP):
+            peer = group * GROUP + q
+
+            @pl.when(peer != me)
+            def _():
+                exchange(2, gathered.at[peer], gathered, peer, peer).wait_recv()
+
+        for q in range(GROUP):
+            peer = group * GROUP + q
+            at = pl.ds(pl.multiple_of(peer * width, width), width)
+            stream = gathered[peer] + residual[:, at].astype(f32)
+            squares = squares + stream * stream
+            scaled_ref[group, :, q * width : (q + 1) * width] = (
+                stream * gain[at].astype(f32).reshape(1, width)
+            ).astype(bf16)
+        scaled = scaled_ref[group]
+        at = pl.ds(pl.multiple_of(group * span, span), span)
+        logits = logits + lax.dot_general(
+            scaled, router[:, at], (((1,), (1,)), ((), ())), preferred_element_type=f32
+        )
+        acc_gate[...] += jnp.dot(scaled, w_gate[at, :], preferred_element_type=f32)
+        acc_up[...] += jnp.dot(scaled, w_up[at, :], preferred_element_type=f32)
+        return squares, logits
+
+    acc_gate[...] = jnp.zeros_like(acc_gate)
+    acc_up[...] = jnp.zeros_like(acc_up)
+    squares, logits = lax.fori_loop(
+        0, groups, absorb, (jnp.zeros((seqs, width), f32), jnp.zeros(logit_shape, f32))
+    )
     inv_rms = lax.rsqrt(jnp.sum(squares, axis=1, keepdims=True) / (n * width) + 1e-05)
-    for p in range(n):
-        at = slice(p * width, (p + 1) * width)
-        normed_ref[:, at] = (stream[p] * inv_rms * gain[:, at].astype(f32)).astype(bf16)
-
-    normed = normed_ref[...]
-    logits = lax.dot_general(
-        normed, router[...], (((1,), (1,)), ((), ())), preferred_element_type=f32
-    )
+    gate_part = acc_gate[...] * inv_rms
+    hidden_ref[...] = (gate_part / (1.0 + jnp.exp(-gate_part)) * (acc_up[...] * inv_rms)).astype(bf16)
+
+    logits = logits * inv_rms
     expert = lax.broadcasted_iota(jnp.int32, logits.shape, 1)
     token = lax.broadcasted_iota(jnp.int32, (seqs, 1), 0)
     first_id = jnp.zeros((seqs, 1), jnp.int32)
     second_id = jnp.zeros((seqs, 1), jnp.int32)
     for b in range(seqs):
-        first_id = jnp.where(token == b, ids_ref[b, 0], first_id)
-        second_id = jnp.where(token == b, ids_ref[b, 1], second_id)
+        first_id = jnp.where(token == b, ids_ref[0, b], first_id)
+        second_id = jnp.where(token == b, ids_ref[1, b], second_id)
     first_logit = jnp.sum(jnp.where(expert == first_id, logits, 0.0), axis=1, keepdims=True)
     second_logit = jnp.sum(jnp.where(expert == second_id, logits, 0.0), axis=1, keepdims=True)
     first_gate = 1.0 / (1.0 + jnp.exp(second_logit - first_logit))
@@ -399,35 +440,25 @@
     route = jnp.where(first_id == own_expert, first_gate, 0.0) + jnp.where(
         second_id == own_expert, 1.0 - first_gate, 0.0
     )
-
-    for copies in big[:2]:
-        for copy in copies:
-            copy.wait()
-    tile = 256
-
-    def hidden_step(j, carry):
-        at = pl.ds(pl.multiple_of(j * tile, tile), tile)
-        gate_part = jnp.dot(normed_ref[...], w_gate[:, at], preferred_element_type=f32)
-        up_part = jnp.dot(normed_ref[...], w_up[:, at], preferred_element_type=f32)
-        hidden_ref[:, at] = (gate_part / (1.0 + jnp.exp(-gate_part)) * up_part).astype(bf16)
-        return carry
-
-    lax.fori_loop(0, ff_local // tile, hidden_step, 0)
     for copy in big[2]:
         copy.wait()
 
-    def contribution(peer):
-        at = pl.ds(pl.multiple_of(peer * width, width), width)
-        return jnp.dot(hidden_ref[...], w_down[:, at], preferred_element_type=f32) * route
-
-    def send_contribution(i, carry):
-        peer = lax.rem(me + i, n)
-        send_moe[peer] = contribution(peer)
-        exchange(3, send_moe.at[peer], recv_moe, peer, me).start()
+    def send_contributions(i, carry):
+        group = xor_index(own_group, groups - 1 - i, groups)
+        at = pl.ds(pl.multiple_of(group * span, span), span)
+        terms = jnp.dot(hidden_ref[...], w_down[:, at], preferred_element_type=f32) * route
+        for q in range(GROUP):
+            peer = group * GROUP + q
+            send_moe[peer] = terms[:, q * width : (q + 1) * width]
+
+            @pl.when(peer != me)
+            def _():
+                exchange(3, send_moe.at[peer], recv_moe, peer, me).start()
+
         return carry
 
-    lax.fori_loop(1, n, send_contribution, 0)
-    recv_moe[me] = contribution(me)
+    lax.fori_loop(0, groups, send_contributions, 0)
+    recv_moe[pl.ds(me, 1)] = send_moe[pl.ds(me, 1)]
     wait_all(3, recv_moe)
     layer_out[...] = (stream_own + jnp.sum(recv_moe[...], axis=0)).astype(bf16)
 
@@ -440,6 +471,11 @@
         return carry
 
     lax.fori_loop(1, n, finish, 0)
+
+
+def emit_kernel(attn_ref, layer_ref, attn_out, layer_out):
+    attn_out[...] = attn_ref[...]
+    layer_out[...] = layer_ref[...]
 
 
 def fused_device(n, *args):
@@ -461,7 +497,7 @@
     ) = args
     seqs, features = residual_input.shape
     width = w_out.shape[0]
-    if width % HEAD_DIM or w_gate.shape[1] % 256 or width * n != features or cache_keys.shape[1] % 16:
+    if n < 2 * GROUP or n & (n - 1) or width % HEAD_DIM or FF % w_gate.shape[1] or width * n != features or cache_keys.shape[1] % 16:
         return per_device(*args)
     f32, bf16 = jnp.float32, jnp.bfloat16
     operands = (
@@ -472,7 +508,7 @@
         cache_values,
         residual_input,
         w_out,
-        norm_gain.reshape(1, features),
+        norm_gain,
         w_router.T,
         w_gate,
         w_up,
@@ -481,7 +517,7 @@
     packet = (n, seqs, width + HEAD_DIM)
     block = (n, seqs, width)
     out = jax.ShapeDtypeStruct((seqs, width), bf16)
-    return pl.pallas_call(
+    results = pl.pallas_call(
         functools.partial(layer_kernel, n),
         out_shape=(out, out),
         in_specs=[pl.BlockSpec(memory_space=pltpu.SMEM)] * 2
@@ -496,7 +532,9 @@
             pltpu.VMEM(block, f32),
             pltpu.VMEM(block, f32),
             pltpu.VMEM(block, f32),
-            pltpu.VMEM((seqs, features), bf16),
+            pltpu.VMEM((n // GROUP, seqs, GROUP * width), bf16),
+            pltpu.VMEM((seqs, w_gate.shape[1]), f32),
+            pltpu.VMEM((seqs, w_gate.shape[1]), f32),
             pltpu.VMEM((seqs, w_gate.shape[1]), bf16),
             pltpu.SemaphoreType.DMA((9,)),
             pltpu.SemaphoreType.DMA((4,)),
@@ -508,7 +546,13 @@
         compiler_params=pltpu.CompilerParams(
             collective_id=0, has_side_effects=True, vmem_limit_bytes=60 * 1024 * 1024
         ),
-    )(cache_lengths, expert_ids, *operands)
+    )(cache_lengths, expert_ids.T, *operands)
+    return pl.pallas_call(
+        emit_kernel,
+        out_shape=(out, out),
+        in_specs=[pl.BlockSpec(memory_space=pltpu.VMEM)] * 2,
+        out_specs=(pl.BlockSpec(memory_space=pltpu.VMEM),) * 2,
+    )(*results)
 
 
 def solution(mesh):

time: 43.7 us -> 36.6 us (0.84)
  local copies, waits for them, and re-layouts: 5.19 us -> 0 us
  Pallas kernels: 37.6 us -> 35.8 us
    unnamed x3 -> x0, local copies, waits for them, and re-layouts: 3.88 us -> none
    pallas_call x1, Pallas kernels: 37.6 us -> 34.5 us  [fused_device(): pl.pallas_call(functools.partial(layer_kernel, n), out_shape=(out, out),...]
    reshape x1 -> x0, local copies, waits for them, and re-layouts: 1.31 us -> none  [fused_device(): norm_gain.reshape(1, features)]
    pallas_call x0 -> x1, Pallas kernels: none -> 1.3 us  [fused_device(): pl.pallas_call(emit_kernel, out_shape=(out, out), in_specs=[pl.BlockSpec(...]
where the time goes in v2:
time: 36.6 us; the launch traced here: 36.4 us
  Pallas kernels  35.8 us (98%)
  between operations  0.64 us (2%)
    pallas_call x1, Pallas kernels, fused_device(): pl.pallas_call(functools.partial(layer_kernel, n), out_shape=(out, out),...  34.5 us
    pallas_call x1, Pallas kernels, fused_device(): pl.pallas_call(emit_kernel, out_shape=(out, out), in_specs=[pl.BlockSpec(...  1.3 us

profile of v2, /device:TPU:0, one launch (start us, length us, event | category | flops | bytes accessed | tf_op | source)
XLA Modules:
  0.0 36.4 jit_solution(2845554195354331558)
XLA Ops:
  0.6 34.5 %shard_map.149 = (bf16[8,256]{1,0:T(8,128)(2,1)}, bf16[8,256]{1,0:T(8,128)(2,1)}) custom-call(s32[8]{0:T(128)} %lengths_ref.1, s32[2,8]{1,0:T(2,128)} %bitcast.3, bf16[8,4096]{1,0:T(8,128)(2,1)} %query_hbm.1, bf16[8,1024]{1,0:T(8,128)(2,1)} %new_key_hbm.1, bf16[8,1024]{1,0:T(8,128)(2,1)} %new_value_hbm.1, bf16[8,64,1024]{2,1,0:T(8,128)(2,1)} %keys_hbm.1, ...), custom_call_target="tpu_custom_call" | custom-call | tf_op jit(solution)/shard_map/pallas_call | solution.py:520
  35.1 1.3 %shard_map.150 = (bf16[8,256]{1,0:T(8,128)(2,1)}, bf16[8,256]{1,0:T(8,128)(2,1)}) custom-call(bf16[8,256]{1,0:T(8,128)(2,1)} %get-tuple-element.4.attn_ref, bf16[8,256]{1,0:T(8,128)(2,1)} %get-tuple-element.5.layer_ref), custom_call_target="tpu_custom_call" | custom-call | tf_op jit(solution)/shard_map/pallas_call | solution.py:550
